TPU v7x, 512 devices: a whole 4x8x8 slice. The times are simulated.
512 devices in a mesh: bank: 64 (over z, x, core), zero: 8 (over y).
Axes of the slice: x: 4, y: 8, z: 8, core: 2. Of those that a mesh axis runs over, the one named last changes fastest.
Arguments:
- master_down: float32 [64, 1408, 2048], P('bank', None, 'zero'), may hold values from -0.21875 to 0.21875
- second_down: bfloat16 [64, 1408, 2048], P('bank', None, 'zero'), may hold values from -0.078125 to 0.078125
- router_weight: float32 [2048, 64], P('zero', 'bank'), may hold values from -0.125 to 0.125
- router_gain: float32 [2048], P('zero'), may hold values from 0.25 to 1.75
Outputs:
- final_down: bfloat16 [64, 1408, 2048], P('bank')
- scale_down: float32 [64, 1408], P('bank')
- serve_router: bfloat16 [2048, 64], replicated
All inputs are finite; a program needn't handle non-finite values.
Results may differ from a plain program's by a relative error of at most 0.001.
Values may be sent and summed in bfloat16 or wider, within the bound.
A program may use at most 64 MiB of HBM per device.

v0:
```python
import jax
import jax.numpy as jnp
from jax import lax
from jax.sharding import PartitionSpec as P


def from_everyone(value, axis):
    size = lax.axis_size(axis)
    return lax.all_to_all(
        jnp.broadcast_to(value[None], (size, *value.shape)), axis, 0, 0, tiled=True
    )


def over_copies(value, axis):
    return from_everyone(value, axis).sum(axis=0)


def in_order(pieces, dim):
    dims = list(pieces.shape[1:])
    dims[dim] *= pieces.shape[0]
    return jnp.moveaxis(pieces, 0, dim).reshape(dims)


def collect(value, axis, dim):
    return in_order(from_everyone(value, axis), dim)


def body(master_down, second_down, router_weight, router_gain):
    merged_down = master_down + second_down.astype(jnp.float32)
    total_down = over_copies(jnp.sum(merged_down * merged_down, axis=2), "zero")
    scale_down = jnp.sqrt(total_down)
    narrow_down = (merged_down / jnp.expand_dims(scale_down, 2)).astype(jnp.bfloat16)
    final_down = lax.all_gather(narrow_down, "zero", axis=2, tiled=True)
    part_router = (router_weight * router_gain[:, None]).astype(jnp.bfloat16)
    row_router = lax.all_gather(part_router, "zero", axis=0, tiled=True)
    serve_router = collect(row_router, "bank", 1)
    return (final_down, scale_down, serve_router)


def solution(mesh):
    return jax.shard_map(
        body,
        mesh=mesh,
        in_specs=(P("bank", None, "zero"), P("bank", None, "zero"), P("zero", "bank"), P("zero")),
        out_specs=(P("bank", None, None), P("bank", None), P()),
        check_vma=False,
    )
```

profile of v0, /device:TPU:6, one launch (start us, length us, event | category | flops | bytes accessed | tf_op | source)
XLA Modules:
  0.0 114.9 jit_solution(9346307011874724087)
XLA Ops:
  7.2 0.0 copy-start
  7.2 0.0 copy-start.1
  7.2 0.0 all-gather.2.cloned.1.call-start
  7.2 2.0 %multiply_reduce_fusion = f32[1408]{0:T(1024)S(1)} fusion(f32[1,1408,256]{2,1,0:T(8,128)} %param.4, bf16[1,1408,256]{2,1,0:T(8,128)(2,1)} %param.5), kind=kLoop, calls=%fused_computation.1 | loop fusion | flops 1440384 | bytes 2168320 | tf_op jit(solution)/shard_map/reduce_sum | solution.py:30
  9.2 15.1 %all_to_all.10 = f32[8,1,1408]{2,1,0:T(1,128)S(1)} all-to-all(f32[8,1,1408]{2,1,0:T(1,128)S(1)} %broadcast_in_dim.8), channel_id=1, replica_groups=mesh['bank'=64,'zero'=8] {'zero'}, dimensions={0} | all-to-all | bytes 90112 | tf_op jit(solution)/shard_map/all_to_all | solution.py:9
  24.3 0.0 copy-done
  24.4 0.0 copy-done.1
  24.4 0.0 copy-start.2
  24.4 0.0 copy-start.3
  24.4 1.1 divide_convert_fusion
  25.5 0.0 all-gather.2.cloned.1.call-update
  25.5 0.0 copy-done.2
  25.5 0.0 copy-done.3
  25.6 13.9 %all_gather.7 = bf16[2048,1]{0,1:T(2,128)(2,1)S(1)} all-gather(bf16[256,1]{0,1:T(2,128)(2,1)S(1)} %multiply_convert_fusion), channel_id=1, replica_groups=mesh['bank'=64,'zero'=8] {'zero'}, dimensions={0}, use_global_device_ids=true | all-gather | bytes 4608 | tf_op jit(solution)/shard_map/all_gather | solution.py:35
  39.5 0.3 broadcast_bitcast_fusion
  39.8 0.5 broadcast.5
  40.3 2.2 %reduce.3 = bf16[64,2048]{1,0:T(8,128)(2,1)S(1)} reduce(bf16[64,1,2048]{2,1,0:T(2,128)(2,1)S(1)} %broadcast_bitcast_fusion, bf16[]{:T(256)} %broadcast.5), dimensions={1}, to_apply=%broadcast_bitcast_fusion.reduce_sub_computation | reduce | bytes 524290
  42.4 0.9 reshape.35
  43.3 14.0 %all-to-all-start.1 = ((bf16[64,2,1024]{2,1,0:T(2,128)(2,1)}), bf16[64,2,1024]{2,1,0:T(2,128)(2,1)S(1)}, u32[]{:S(2)}, u32[]{:S(2)}) async-start(bf16[64,2,1024]{2,1,0:T(2,128)(2,1)} %reshape.35), calls=%async_computation.1 | async-start | bytes 524288 | tf_op jit(solution)/shard_map/all_to_all | solution.py:9
  57.3 0.6 sqrt.19
  57.9 11.3 %all-to-all-done.1 = bf16[64,2,1024]{2,1,0:T(2,128)(2,1)S(1)} async-done(((bf16[64,2,1024]{2,1,0:T(2,128)(2,1)}), bf16[64,2,1024]{2,1,0:T(2,128)(2,1)S(1)}, u32[]{:S(2)}, u32[]{:S(2)}) %all-to-all-start.1) | async-done | bytes 262176 | tf_op jit(solution)/shard_map/all_to_all | solution.py:9
  69.2 0.2 reshape.36
  69.4 0.9 copy.13
  70.3 31.6 %all-gather.2.cloned.1.call-done = bf16[1,1408,2048]{2,1,0:T(8,128)(2,1)} async-done(((bf16[1,1408,256]{2,1,0:T(8,128)(2,1)}), bf16[1,1408,2048]{2,1,0:T(8,128)(2,1)}) %all-gather.2.cloned.1.call-update) | async-done | bytes 5767184 | tf_op jit(solution)/shard_map/all_gather | solution.py:33
  101.9 6.2 %copy.15 = bf16[1,1408,2048]{2,1,0:T(8,128)(2,1)} copy(bf16[1,1408,2048]{2,1,0:T(8,128)(2,1)} %all-gather.2.cloned.1.call-done) | data formatting | bytes 11534336
  (5 shorter events, 0.1 us)
Async XLA Ops:
  7.2 17.2 %copy-start = (f32[1,1408,256]{2,1,0:T(8,128)S(1)}, f32[1,1408,256]{2,1,0:T(8,128)}, u32[]{:S(2)}) copy-start(f32[1,1408,256]{2,1,0:T(8,128)} %param.4) | copy-start | bytes 4325380
  7.2 17.2 %copy-start.1 = (bf16[1,1408,256]{2,1,0:T(8,128)(2,1)S(1)}, bf16[1,1408,256]{2,1,0:T(8,128)(2,1)}, u32[]{:S(2)}) copy-start(bf16[1,1408,256]{2,1,0:T(8,128)(2,1)} %param.5) | copy-start | bytes 2162692
  7.2 94.8 %all-gather.2.cloned.1.call-start = ((), (), s32[]{:S(2)}) async-start(), calls=%async_computation.2 | async-start | bytes 6488064 | tf_op jit(solution)/shard_map/all_gather | solution.py:33
  24.4 1.2 %copy-start.2 = (f32[256,1]{0,1:T(1,128)S(1)}, f32[256,1]{0,1:T(1,128)}, u32[]{:S(2)}) copy-start(f32[256,1]{0,1:T(1,128)} %param.6) | copy-start | bytes 3076
  24.4 1.2 %copy-start.3 = (f32[256]{0:T(256)S(1)}, f32[256]{0:T(256)}, u32[]{:S(2)}) copy-start(f32[256]{0:T(256)} %param.7) | copy-start | bytes 3076
  43.3 25.9 %all-to-all-start.1 = ((bf16[64,2,1024]{2,1,0:T(2,128)(2,1)}), bf16[64,2,1024]{2,1,0:T(2,128)(2,1)S(1)}, u32[]{:S(2)}, u32[]{:S(2)}) async-start(bf16[64,2,1024]{2,1,0:T(2,128)(2,1)} %reshape.35), calls=%async_computation.1 | async-start | bytes 524288 | tf_op jit(solution)/shard_map/all_to_all | solution.py:9
Sparse Core Ops, SparseCore 0:
  25.6 76.2 all-gather.1
where the time goes:
time: 115 us
  waiting for transfers between devices  43 us (37%)
  blocking collectives  28.9 us (25%)
  between operations  14.1 us (12%)
  starting transfers between devices  14 us (12%)
  local copies, waits for them, and re-layouts  9.55 us (8%)
  other arithmetic  5.32 us (5%)
    all_gather x1, waiting for transfers between devices, body(): final_down = lax.all_gather(narrow_down, 'zero', axis=2, tiled=True)  31.6 us
    all_to_all x1, blocking collectives, from_everyone(): lax.all_to_all(jnp.broadcast_to(value[None], (size, *value.shape)), axis,...  15.1 us
    all_to_all x1, starting transfers between devices, from_everyone(): lax.all_to_all(jnp.broadcast_to(value[None], (size, *value.shape)), axis,...  14 us
    all_gather x1, blocking collectives, body(): row_router = lax.all_gather(part_router, 'zero', axis=0, tiled=True)  13.9 us
    all_to_all x1, waiting for transfers between devices, from_everyone(): lax.all_to_all(jnp.broadcast_to(value[None], (size, *value.shape)), axis,...  11.3 us
    unnamed x13, local copies, waits for them, and re-layouts  8.07 us
  transfers between devices with their start and end apart: 2, of which 2 were waited for; matrix products, arithmetic and copies ran while one was open for 5% of the time, Pallas kernels for 0%

commit v1 on v0

v1 whole, which is shorter than its diff:
```python
import functools

import jax
import jax.numpy as jnp
from jax import lax
from jax.experimental import pallas as pl
from jax.experimental.pallas import tpu as pltpu
from jax.sharding import PartitionSpec as P

MESH = pl.DeviceIdType.MESH
BLOCK = 128
CHUNK = 176
X, CORES = 4, 2


def kernel(
    master, second, weight, gain,
    final, scale, router,
    merged, added, inverse, own_sum, sums, w_v, g_v, part, column, table,
    load_sem, small_sem, local_sem,
    sum_send, sum_recv, ring_send, ring_recv,
    part_send, part_recv, table_send, table_recv,
):
    rows, cols = merged.shape
    zero = lax.axis_size("zero")
    blocks, chunks = rows // BLOCK, rows // CHUNK
    half = chunks // 2
    y, bank = lax.axis_index("zero"), lax.axis_index("bank")
    chip_z, chip_x = bank // (X * CORES), lax.rem(bank // CORES, X)
    depth = lax.axis_size("bank") // (X * CORES)
    core = lax.rem(bank, CORES)

    def at_core(k):
        return bank - core + lax.rem(core + k, CORES)

    def at_x(k):
        return (chip_z * X + lax.rem(chip_x + k, X)) * CORES + core

    def at_z(k):
        return (lax.rem(chip_z + k, depth) * X + chip_x) * CORES + core

    def load(i):
        at = pl.ds(i * BLOCK, BLOCK)
        return (
            pltpu.make_async_copy(master.at[at], merged.at[at], load_sem.at[0, i]),
            pltpu.make_async_copy(second.at[at], added.at[at], load_sem.at[1, i]),
        )

    small = (
        pltpu.make_async_copy(weight, w_v, small_sem.at[0]),
        pltpu.make_async_copy(gain, g_v, small_sem.at[1]),
    )
    for copy in small:
        copy.start()
    for i in range(blocks):
        for copy in load(i):
            copy.start()

    barrier = pltpu.get_barrier_semaphore()
    peers = [{"zero": lax.rem(y + k, zero)} for k in range(1, zero)]
    peers += [{"bank": at_core(1)}]
    peers += [{"bank": at_x(k)} for k in range(1, X)]
    peers += [{"bank": at_z(k)} for k in range(1, depth)]
    for peer in peers:
        pl.semaphore_signal(barrier, inc=1, device_id=peer, device_id_type=MESH)

    for copy in small:
        copy.wait()
    part[...] = (w_v[...] * g_v[...]).astype(jnp.bfloat16).astype(jnp.float32)

    for i in range(blocks):
        at = pl.ds(i * BLOCK, BLOCK)
        for copy in load(i):
            copy.wait()
        value = merged[at] + added[at].astype(jnp.float32)
        merged[at] = value
        square = value * value
        lanes = square[:, :128]
        for j in range(128, cols, 128):
            lanes = lanes + square[:, j : j + 128]
        own_sum[:, at] = jnp.sum(lanes.T, axis=0, keepdims=True)
    sums[y] = own_sum[...]

    pl.semaphore_wait(barrier, len(peers))

    def send_sum(k):
        return pltpu.make_async_remote_copy(
            own_sum, sums.at[y], sum_send.at[k - 1], sum_recv.at[k - 1],
            device_id={"zero": lax.rem(y + k, zero)}, device_id_type=MESH,
        )

    def send_part(k):
        return pltpu.make_async_remote_copy(
            part, column.at[y], part_send.at[k - 1], part_recv.at[k - 1],
            device_id={"zero": lax.rem(y + k, zero)}, device_id_type=MESH,
        )

    for k in (4, 3, 5, 2, 6, 1, 7):
        send_sum(k).start()
    for k in range(1, zero):
        send_part(k).start()
    own_part = pltpu.make_async_copy(part, column.at[y], local_sem.at[0])
    own_part.start()

    for k in range(1, zero):
        send_sum(k).wait_recv()
    total = jnp.sqrt(jnp.sum(sums[...], axis=0))
    scale[...] = total
    own_sum_inverse = 1.0 / total
    for i in range(blocks):
        at = slice(i * BLOCK, (i + 1) * BLOCK)
        inverse[at] = jnp.broadcast_to(own_sum_inverse[:, at], (BLOCK, BLOCK)).T

    def ring(way, hop, c):
        step = 1 if way == 0 else zero - 1
        owner = lax.rem(y + (zero - step) * hop, zero)
        at = final.at[pl.ds(c * CHUNK, CHUNK), pl.ds(pl.multiple_of(owner * cols, cols), cols)]
        return pltpu.make_async_remote_copy(
            at, at, ring_send.at[way, hop, c], ring_recv.at[way, hop, c],
            device_id={"zero": lax.rem(y + step, zero)}, device_id_type=MESH,
        )

    mine = pl.ds(pl.multiple_of(y * cols, cols), cols)

    def own(c, _):
        at = pl.ds(pl.multiple_of(c * CHUNK, CHUNK), CHUNK)
        wide = jnp.concatenate([inverse[at]] * (cols // 128), axis=1)
        final[at, mine] = (merged[at] * wide).astype(jnp.bfloat16)

        @pl.when(c > 0)
        def _():
            ring(0, 0, c - 1).start()
            ring(1, 0, c - 1).start()

        return 0

    lax.fori_loop(0, chunks, own, 0)
    ring(0, 0, chunks - 1).start()
    ring(1, 0, chunks - 1).start()

    own_part.wait()
    for k in range(1, zero):
        send_part(k).wait_recv()

    def send_table(sem, rows_at, count, peer):
        at = table.at[pl.ds(rows_at, count)]
        return pltpu.make_async_remote_copy(
            at, at, table_send.at[sem], table_recv.at[sem],
            device_id={"bank": peer}, device_id_type=MESH,
        )

    own_row = pltpu.make_async_copy(column, table.at[bank], local_sem.at[1])
    own_row.start()
    own_row.wait()
    stages = [
        [send_table(0, bank, 1, at_core(1))],
        [send_table(k, bank - core, CORES, at_x(k)) for k in range(1, X)],
        [send_table(X - 1 + k, chip_z * X * CORES, X * CORES, at_z(k)) for k in range(1, depth)],
    ]

    def table_stage(s):
        if s:
            for copy in stages[s - 1]:
                copy.wait_recv()
        if s < len(stages):
            for copy in stages[s]:
                copy.start()
        else:
            width = part.shape[1]
            for j in range(zero):
                router[:, j * width : (j + 1) * width] = table[:, j, 0, :].astype(jnp.bfloat16)

    def relay(hop, ways, first, last):
        def step(c, _):
            for way in (0, 1):
                ring(way, hop - 1, c).wait_recv()
                if way in ways:
                    ring(way, hop, c).start()
            return 0

        lax.fori_loop(first, last, step, 0)

    table_stage(0)
    relay(1, (0, 1), 0, half)
    table_stage(1)
    relay(1, (0, 1), half, chunks)
    table_stage(2)
    relay(2, (0, 1), 0, chunks)
    table_stage(3)
    relay(3, (0,), 0, half)
    relay(3, (1,), half, chunks)

    def last_cw(c, _):
        ring(0, 3, c).wait_recv()
        ring(1, 3, c + half).wait_recv()
        return 0

    lax.fori_loop(0, half, last_cw, 0)

    def sent(c, _):
        for hop in range(3):
            for way in (0, 1):
                ring(way, hop, c).wait_send()
        return 0

    lax.fori_loop(0, chunks, sent, 0)

    def sent_last(c, _):
        ring(0, 3, c).wait_send()
        ring(1, 3, c + half).wait_send()
        return 0

    lax.fori_loop(0, half, sent_last, 0)
    for k in range(1, zero):
        send_sum(k).wait_send()
        send_part(k).wait_send()
    for stage in stages:
        for copy in stage:
            copy.wait_send()


def in_hbm(value):
    return pltpu.with_memory_space_constraint(value, pltpu.HBM)


def body(master_down, second_down, router_weight, router_gain):
    _, rows, cols = master_down.shape
    width = router_weight.shape[0]
    zero, banks = lax.axis_size("zero"), lax.axis_size("bank")
    blocks, chunks = rows // BLOCK, rows // CHUNK
    depth = banks // (X * CORES)
    f32, vmem, dma = jnp.float32, pltpu.VMEM, pltpu.SemaphoreType.DMA
    final, scale, router = pl.pallas_call(
        kernel,
        out_shape=(
            jax.ShapeDtypeStruct((rows, zero * cols), jnp.bfloat16),
            jax.ShapeDtypeStruct((1, rows), f32),
            jax.ShapeDtypeStruct((banks, zero * width), jnp.bfloat16),
        ),
        in_specs=[pl.BlockSpec(memory_space=pltpu.HBM)] * 4,
        out_specs=[pl.BlockSpec(memory_space=vmem)] * 3,
        scratch_shapes=[
            vmem((rows, cols), f32),
            vmem((rows, cols), jnp.bfloat16),
            vmem((rows, 128), f32),
            vmem((1, rows), f32),
            vmem((zero, 1, rows), f32),
            vmem((1, width), f32),
            vmem((1, width), f32),
            vmem((1, width), f32),
            vmem((zero, 1, width), f32),
            vmem((banks, zero, 1, width), f32),
            dma((2, blocks)),
            dma((2,)),
            dma((2,)),
            dma((zero - 1,)),
            dma((zero - 1,)),
            dma((2, 4, chunks)),
            dma((2, 4, chunks)),
            dma((zero - 1,)),
            dma((zero - 1,)),
            dma((X - 1 + depth,)),
            dma((X - 1 + depth,)),
        ],
        compiler_params=pltpu.CompilerParams(
            collective_id=0, has_side_effects=True, vmem_limit_bytes=40 * 2**20
        ),
        name="gather",
    )(
        in_hbm(master_down.reshape(rows, cols)),
        in_hbm(second_down.reshape(rows, cols)),
        in_hbm(router_weight.reshape(1, width)),
        in_hbm(router_gain.reshape(1, width)),
    )
    return final.reshape(1, rows, zero * cols), scale, router.T


def solution(mesh):
    return jax.shard_map(
        body,
        mesh=mesh,
        in_specs=(P("bank", None, "zero"), P("bank", None, "zero"), P("zero", "bank"), P("zero")),
        out_specs=(P("bank", None, None), P("bank", None), P()),
        check_vma=False,
    )
```

time: 115 us -> 79 us (0.69)
  Pallas kernels: 0 us -> 74.3 us
  waiting for transfers between devices: 43 us -> 0 us
  blocking collectives: 28.9 us -> 0 us
  starting transfers between devices: 14 us -> 0 us
  between operations: 14.1 us -> 0.64 us
  local copies, waits for them, and re-layouts: 9.55 us -> 3.83 us
  other arithmetic: 5.32 us -> 0 us
    pallas_call x0 -> x1, Pallas kernels: none -> 74.3 us  [body(): pl.pallas_call(kernel, out_shape=(jax.ShapeDtypeStruct((rows, zero * cols...]
    all_gather x1 -> x0, waiting for transfers between devices: 31.6 us -> none  [body(): final_down = lax.all_gather(narrow_down, 'zero', axis=2, tiled=True)]
    all_to_all x1 -> x0, blocking collectives: 15.1 us -> none  [from_everyone(): lax.all_to_all(jnp.broadcast_to(value[None], (size, *value.shape)), axis,...]
    all_to_all x1 -> x0, starting transfers between devices: 14 us -> none  [from_everyone(): lax.all_to_all(jnp.broadcast_to(value[None], (size, *value.shape)), axis,...]
    all_gather x1 -> x0, blocking collectives: 13.9 us -> none  [body(): row_router = lax.all_gather(part_router, 'zero', axis=0, tiled=True)]
    all_to_all x1 -> x0, waiting for transfers between devices: 11.3 us -> none  [from_everyone(): lax.all_to_all(jnp.broadcast_to(value[None], (size, *value.shape)), axis,...]
    unnamed x13 -> x3, local copies, waits for them, and re-layouts: 8.07 us -> 3.83 us
    unnamed x1 -> x0, other arithmetic: 2.15 us -> none
  transfers between devices with their start and end apart: 2 -> 0, of which waited for: 2 -> 0; matrix products, arithmetic and copies ran while one was open for 5% -> 0% of each run, Pallas kernels for 0% -> 0%
where the time goes in v1:
time: 79 us; the launch traced here: 78.8 us
  Pallas kernels  74.3 us (94%)
  local copies, waits for them, and re-layouts  3.83 us (5%)
    pallas_call x1, Pallas kernels, body(): pl.pallas_call(kernel, out_shape=(jax.ShapeDtypeStruct((rows, zero * cols...  74.3 us
    unnamed x3, local copies, waits for them, and re-layouts  3.83 us

profile of v1, /device:TPU:6, one launch (start us, length us, event | category | flops | bytes accessed | tf_op | source)
XLA Modules:
  0.0 78.8 jit_solution(13909099122815273284)
XLA Ops:
  0.6 74.3 %gather.1 = (bf16[1408,2048]{1,0:T(8,128)(2,1)S(1)}, f32[1,1408]{1,0:T(1,128)S(1)}, bf16[64,2048]{1,0:T(8,128)(2,1)S(1)}) custom-call(f32[1408,256]{1,0:T(8,128)} %bitcast.8, bf16[1408,256]{1,0:T(8,128)(2,1)} %bitcast.9, f32[1,256]{1,0:T(1,128)} %bitcast.10, f32[1,256]{1,0:T(1,128)} %bitcast.11), custom_call_target="tpu_custom_call" | custom-call | tf_op jit(solution)/shard_map/gather/pallas_call | solution.py:233
  75.0 2.5 %copy.10 = bf16[1,1408,2048]{2,1,0:T(8,128)(2,1)} copy(bf16[1,1408,2048]{2,1,0:T(8,128)(2,1)S(1)} %bitcast.6) | data formatting | bytes 11534336
  77.5 0.6 copy.11
  78.1 0.7 copy.12

commit v2 on v1

--- a/solution.py
+++ b/solution.py
@@ -9,15 +9,16 @@
 
 MESH = pl.DeviceIdType.MESH
 BLOCK = 128
-CHUNK = 176
+CHUNK = 88
+EARLY = 1
 X, CORES = 4, 2
 
 
 def kernel(
     master, second, weight, gain,
     final, scale, router,
-    merged, added, inverse, own_sum, sums, w_v, g_v, part, column, table,
-    load_sem, small_sem, local_sem,
+    merged, added, inverse, own_sum, sums, w_v, g_v, part, column, table, early,
+    ready, opened, early_send, early_recv, load_sem, small_sem, local_sem,
     sum_send, sum_recv, ring_send, ring_recv,
     part_send, part_recv, table_send, table_recv,
 ):
@@ -57,12 +58,20 @@
             copy.start()
 
     barrier = pltpu.get_barrier_semaphore()
-    peers = [{"zero": lax.rem(y + k, zero)} for k in range(1, zero)]
-    peers += [{"bank": at_core(1)}]
-    peers += [{"bank": at_x(k)} for k in range(1, X)]
-    peers += [{"bank": at_z(k)} for k in range(1, depth)]
-    for peer in peers:
-        pl.semaphore_signal(barrier, inc=1, device_id=peer, device_id_type=MESH)
+
+    def signal(sem, peer):
+        pl.semaphore_signal(sem, inc=1, device_id=peer, device_id_type=MESH)
+
+    for k in range(1, zero):
+        peer = lax.rem(y + k, zero)
+
+        @pl.when(peer != 0)
+        def _(peer=peer):
+            signal(barrier, {"zero": peer})
+
+    others = [at_core(1)]
+    others += [at_x(k) for k in range(1, X)]
+    others += [at_z(k) for k in range(1, depth)]
 
     for copy in small:
         copy.wait()
@@ -81,7 +90,17 @@
         own_sum[:, at] = jnp.sum(lanes.T, axis=0, keepdims=True)
     sums[y] = own_sum[...]
 
-    pl.semaphore_wait(barrier, len(peers))
+    @pl.when(y != 0)
+    def _():
+        pl.semaphore_wait(barrier, zero - 1)
+
+    @pl.when(y == 1)
+    def _():
+        signal(ready, {"zero": 0})
+
+    @pl.when(y == 0)
+    def _():
+        pl.semaphore_wait(ready, 1)
 
     def send_sum(k):
         return pltpu.make_async_remote_copy(
@@ -95,10 +114,25 @@
             device_id={"zero": lax.rem(y + k, zero)}, device_id_type=MESH,
         )
 
+    def send_early(way):
+        peer = lax.rem(y + (1 if way == 0 else zero - 1), zero)
+        return pltpu.make_async_remote_copy(
+            merged.at[pl.ds(0, EARLY * CHUNK)], early.at[way], early_send.at[way], early_recv.at[way],
+            device_id={"zero": peer}, device_id_type=MESH,
+        )
+
     for k in (4, 3, 5, 2, 6, 1, 7):
         send_sum(k).start()
+    for way in (0, 1):
+        send_early(way).start()
     for k in range(1, zero):
         send_part(k).start()
+
+    @pl.when(y == 0)
+    def _():
+        for peer in others:
+            signal(barrier, {"bank": peer})
+
     own_part = pltpu.make_async_copy(part, column.at[y], local_sem.at[0])
     own_part.start()
 
@@ -120,23 +154,57 @@
             device_id={"zero": lax.rem(y + step, zero)}, device_id_type=MESH,
         )
 
-    mine = pl.ds(pl.multiple_of(y * cols, cols), cols)
-
-    def own(c, _):
+    def narrow(source, c, owner):
         at = pl.ds(pl.multiple_of(c * CHUNK, CHUNK), CHUNK)
         wide = jnp.concatenate([inverse[at]] * (cols // 128), axis=1)
-        final[at, mine] = (merged[at] * wide).astype(jnp.bfloat16)
-
-        @pl.when(c > 0)
+        final[at, pl.ds(pl.multiple_of(owner * cols, cols), cols)] = (source[at] * wide).astype(jnp.bfloat16)
+
+    def own(c, _):
+        narrow(merged, c, y)
+
+        @pl.when(c > EARLY)
         def _():
             ring(0, 0, c - 1).start()
             ring(1, 0, c - 1).start()
 
         return 0
 
-    lax.fori_loop(0, chunks, own, 0)
+    lax.fori_loop(EARLY, chunks, own, 0)
+
+    def own_early(c, _):
+        narrow(merged, c, y)
+        return 0
+
+    lax.fori_loop(0, EARLY, own_early, 0)
     ring(0, 0, chunks - 1).start()
     ring(1, 0, chunks - 1).start()
+
+    for way in (0, 1):
+        send_early(way).wait_recv()
+    left, right = lax.rem(y + zero - 1, zero), lax.rem(y + 1, zero)
+
+    def neighbours_early(c, _):
+        narrow(early.at[0], c, left)
+        narrow(early.at[1], c, right)
+
+        @pl.when(c > 0)
+        def _():
+            ring(0, 1, c - 1).start()
+            ring(1, 1, c - 1).start()
+
+        return 0
+
+    lax.fori_loop(0, EARLY, neighbours_early, 0)
+
+    @pl.when(y == 0)
+    def _():
+        pl.semaphore_wait(barrier, len(others))
+        for k in range(1, zero):
+            signal(opened, {"zero": k})
+
+    @pl.when(y != 0)
+    def _():
+        pl.semaphore_wait(opened, 1)
 
     own_part.wait()
     for k in range(1, zero):
@@ -180,8 +248,10 @@
 
         lax.fori_loop(first, last, step, 0)
 
+    ring(0, 1, EARLY - 1).start()
+    ring(1, 1, EARLY - 1).start()
     table_stage(0)
-    relay(1, (0, 1), 0, half)
+    relay(1, (0, 1), EARLY, half)
     table_stage(1)
     relay(1, (0, 1), half, chunks)
     table_stage(2)
@@ -197,12 +267,20 @@
 
     lax.fori_loop(0, half, last_cw, 0)
 
+    def sent_first(c, _):
+        for way in (0, 1):
+            ring(way, 0, c).wait_send()
+        return 0
+
     def sent(c, _):
-        for hop in range(3):
+        for hop in (1, 2):
             for way in (0, 1):
                 ring(way, hop, c).wait_send()
         return 0
 
+    for way in (0, 1):
+        send_early(way).wait_send()
+    lax.fori_loop(EARLY, chunks, sent_first, 0)
     lax.fori_loop(0, chunks, sent, 0)
 
     def sent_last(c, _):
@@ -217,6 +295,20 @@
     for stage in stages:
         for copy in stage:
             copy.wait_send()
+
+
+def write(final, scale, router, final_out, scale_out, router_out, sem):
+    copies = [
+        pltpu.make_async_copy(scale, scale_out, sem.at[0]),
+        pltpu.make_async_copy(router, router_out, sem.at[1]),
+    ]
+    for i in range(final.shape[0] // BLOCK):
+        at = pl.ds(i * BLOCK, BLOCK)
+        copies.append(pltpu.make_async_copy(final.at[at], final_out.at[at], sem.at[2 + i]))
+    for copy in copies:
+        copy.start()
+    for copy in copies:
+        copy.wait()
 
 
 def in_hbm(value):
@@ -250,6 +342,11 @@
             vmem((1, width), f32),
             vmem((zero, 1, width), f32),
             vmem((banks, zero, 1, width), f32),
+            vmem((2, EARLY * CHUNK, cols), f32),
+            pltpu.SemaphoreType.REGULAR,
+            pltpu.SemaphoreType.REGULAR,
+            dma((2,)),
+            dma((2,)),
             dma((2, blocks)),
             dma((2,)),
             dma((2,)),
@@ -272,6 +369,15 @@
         in_hbm(router_weight.reshape(1, width)),
         in_hbm(router_gain.reshape(1, width)),
     )
+    final, scale, router = pl.pallas_call(
+        write,
+        out_shape=tuple(jax.ShapeDtypeStruct(x.shape, x.dtype) for x in (final, scale, router)),
+        in_specs=[pl.BlockSpec(memory_space=pl.ANY)] * 3,
+        out_specs=[pl.BlockSpec(memory_space=pl.ANY)] * 3,
+        scratch_shapes=[dma((blocks + 2,))],
+        compiler_params=pltpu.CompilerParams(vmem_limit_bytes=2**20),
+        name="write",
+    )(*(pltpu.with_memory_space_constraint(x, vmem) for x in (final, scale, router)))
     return final.reshape(1, rows, zero * cols), scale, router.T
 
 

time: 79 us -> 72.2 us (0.914)
  local copies, waits for them, and re-layouts: 3.83 us -> 0 us
  Pallas kernels: 74.3 us -> 71.4 us
    pallas_call x1, Pallas kernels: 74.3 us -> 68.7 us  [body(): pl.pallas_call(kernel, out_shape=(jax.ShapeDtypeStruct((rows, zero * cols...]
    unnamed x3 -> x0, local copies, waits for them, and re-layouts: 3.83 us -> none
    pallas_call x0 -> x1, Pallas kernels: none -> 2.69 us  [body(): pl.pallas_call(write, out_shape=tuple((jax.ShapeDtypeStruct(x.shape, x.dt...]
where the time goes in v2:
time: 72.2 us; the launch traced here: 72 us
  Pallas kernels  71.4 us (99%)
    pallas_call x1, Pallas kernels, body(): pl.pallas_call(kernel, out_shape=(jax.ShapeDtypeStruct((rows, zero * cols...  68.7 us
    pallas_call x1, Pallas kernels, body(): pl.pallas_call(write, out_shape=tuple((jax.ShapeDtypeStruct(x.shape, x.dt...  2.69 us

profile of v2, /device:TPU:6, one launch (start us, length us, event | category | flops | bytes accessed | tf_op | source)
XLA Modules:
  0.0 72.0 jit_solution(5553319328690737637)
XLA Ops:
  0.6 68.7 %gather.1 = (bf16[1408,2048]{1,0:T(8,128)(2,1)S(1)}, f32[1,1408]{1,0:T(1,128)S(1)}, bf16[64,2048]{1,0:T(8,128)(2,1)S(1)}) custom-call(f32[1408,256]{1,0:T(8,128)} %bitcast.6, bf16[1408,256]{1,0:T(8,128)(2,1)} %bitcast.7, f32[1,256]{1,0:T(1,128)} %bitcast.8, f32[1,256]{1,0:T(1,128)} %bitcast.9), custom_call_target="tpu_custom_call" | custom-call | tf_op jit(solution)/shard_map/gather/pallas_call | solution.py:325
  69.3 2.7 %write.1 = (bf16[1408,2048]{1,0:T(8,128)(2,1)}, f32[1,1408]{1,0:T(1,128)}, bf16[64,2048]{1,0:T(8,128)(2,1)}) custom-call(bf16[1408,2048]{1,0:T(8,128)(2,1)S(1)} %get-tuple-element.9.final, f32[1,1408]{1,0:T(1,128)S(1)} %get-tuple-element.10.scale, bf16[64,2048]{1,0:T(8,128)(2,1)S(1)} %get-tuple-element.11.router), custom_call_target="tpu_custom_call" | custom-call | tf_op jit(solution)/shard_map/write/pallas_call | solution.py:372

commit v3 on v0

v3 whole, which is shorter than its diff:
```python
import jax
import jax.numpy as jnp
from jax import lax
from jax.experimental import pallas as pl
from jax.experimental.pallas import tpu as pltpu
from jax.sharding import PartitionSpec as P

MESH = pl.DeviceIdType.MESH
BLOCK = 128
CHUNKS = 4
LOADS = 4
EARLY = 0
X, CORES = 4, 2


def kernel(
    master, second, weight, gain,
    final, scale, router,
    merged, added, own_sum, sums, w_v, g_v, part, column, table, early,
    ready, opened, load_sem, small_sem, local_sem,
    sum_send, sum_recv, part_send, part_recv, table_send, table_recv,
    early_send, early_recv, own_send, relay_send, ring_recv,
):
    rows, cols = merged.shape
    zero = lax.axis_size("zero")
    blocks, chunk, half = rows // BLOCK, rows // CHUNKS, CHUNKS // 2
    y, bank = lax.axis_index("zero"), lax.axis_index("bank")
    chip_z, chip_x = bank // (X * CORES), lax.rem(bank // CORES, X)
    depth = lax.axis_size("bank") // (X * CORES)
    core = lax.rem(bank, CORES)

    def at_core(k):
        return bank - core + lax.rem(core + k, CORES)

    def at_x(k):
        return (chip_z * X + lax.rem(chip_x + k, X)) * CORES + core

    def at_z(k):
        return (lax.rem(chip_z + k, depth) * X + chip_x) * CORES + core

    def signal(sem, peer):
        pl.semaphore_signal(sem, inc=1, device_id=peer, device_id_type=MESH)

    def arrived(ref, sem):
        pltpu.make_async_copy(ref, ref, sem).wait()

    def remote(source, target, send_sem, recv_sem, peer):
        return pltpu.make_async_remote_copy(
            source, target, send_sem, recv_sem, device_id=peer, device_id_type=MESH
        )

    barrier = pltpu.get_barrier_semaphore()
    for k in range(1, zero):
        peer = lax.rem(y + k, zero)

        @pl.when(peer != 0)
        def _(peer=peer):
            signal(barrier, {"zero": peer})

    step = rows // LOADS
    for i in range(LOADS):
        at = pl.ds(i * step, step)
        pltpu.make_async_copy(master.at[at], merged.at[at], load_sem.at[0]).start()
        pltpu.make_async_copy(second.at[at], added.at[at], load_sem.at[1]).start()
    small = (
        pltpu.make_async_copy(weight, w_v, small_sem.at[0]),
        pltpu.make_async_copy(gain, g_v, small_sem.at[1]),
    )
    for copy in small:
        copy.start()

    arrived(merged, load_sem.at[0])
    arrived(added, load_sem.at[1])
    for i in range(blocks):
        at = pl.ds(i * BLOCK, BLOCK)
        value = merged[at] + added[at].astype(jnp.float32)
        merged[at] = value
        square = value * value
        lanes = square[:, :128]
        for j in range(128, cols, 128):
            lanes = lanes + square[:, j : j + 128]
        own_sum[:, at] = jnp.sum(lanes.T, axis=0, keepdims=True)
    sums[y] = own_sum[...]

    for copy in small:
        copy.wait()
    part[...] = (w_v[...] * g_v[...]).astype(jnp.bfloat16).astype(jnp.float32)

    @pl.when(y != 0)
    def _():
        pl.semaphore_wait(barrier, zero - 1)

    @pl.when(y == 1)
    def _():
        signal(ready, {"zero": 0})

    @pl.when(y == 0)
    def _():
        pl.semaphore_wait(ready, 1)

    left, right = lax.rem(y + zero - 1, zero), lax.rem(y + 1, zero)

    def early_rows(way):
        return pl.ds(0 if way == 0 else rows - EARLY * BLOCK, EARLY * BLOCK)

    def send_early(way):
        return remote(
            merged.at[early_rows(way)], early.at[way], early_send.at[way], early_recv.at[way],
            {"zero": right if way == 0 else left},
        )

    for k in (4, 3, 5, 2, 6, 1, 7):
        remote(own_sum, sums.at[y], sum_send, sum_recv, {"zero": lax.rem(y + k, zero)}).start()
    if EARLY:
        for way in (0, 1):
            send_early(way).start()
    for k in range(1, zero):
        remote(part, column.at[y], part_send, part_recv, {"zero": lax.rem(y + k, zero)}).start()
    own_part = pltpu.make_async_copy(part, column.at[y], local_sem)
    own_part.start()

    others = [at_core(1)]
    others += [at_x(k) for k in range(1, X)]
    others += [at_z(k) for k in range(1, depth)]

    @pl.when(y == 0)
    def _():
        for peer in others:
            signal(barrier, {"bank": peer})

    arrived(sums.at[pl.ds(0, zero - 1)], sum_recv)
    total = jnp.sqrt(jnp.sum(sums[...], axis=0))
    scale[...] = total
    inverse = 1.0 / total

    def columns(owner):
        return pl.ds(pl.multiple_of(owner * cols, cols), cols)

    def narrow(source, block, owner):
        at = slice(block * BLOCK, (block + 1) * BLOCK)
        tall = jnp.broadcast_to(inverse[:, at], (BLOCK, BLOCK)).T
        wide = jnp.concatenate([tall] * (cols // 128), axis=1)
        final[at, columns(owner)] = (source[...] * wide).astype(jnp.bfloat16)

    def ring(way, hop, place):
        c = place if way == 0 else CHUNKS - 1 - place
        start, count = c * chunk, chunk
        if hop == 0 and place == 0:
            start, count = start + (EARLY * BLOCK if way == 0 else 0), count - EARLY * BLOCK
        owner = lax.rem(y + (zero - hop if way == 0 else hop), zero)
        at = final.at[pl.ds(start, count), columns(owner)]
        sem = own_send if hop == 0 else relay_send
        return remote(
            at, at, sem.at[way], ring_recv.at[way, hop * CHUNKS + place],
            {"zero": right if way == 0 else left},
        )

    mine = list(range(EARLY, blocks - EARLY))
    order = []
    for place in range(CHUNKS):
        for way in (0, 1):
            c = place if way == 0 else CHUNKS - 1 - place
            need = [i for i in mine if i * BLOCK < (c + 1) * chunk and (i + 1) * BLOCK > c * chunk]
            order.append(([i for i in need if all(i not in o[0] for o in order)], way, place))
    waiting = None
    for need, way, place in order:
        for i in need:
            narrow(merged.at[pl.ds(i * BLOCK, BLOCK)], i, y)
        if waiting and need:
            ring(*waiting).start()
            waiting = None
        elif waiting:
            ring(*waiting).start()
        waiting = (way, 0, place)
    for i in range(blocks):
        if i not in mine:
            narrow(merged.at[pl.ds(i * BLOCK, BLOCK)], i, y)
    ring(*waiting).start()

    if EARLY:
        for way in (0, 1):
            send_early(way).wait_recv()
            for i in range(EARLY):
                first = early_rows(way).start // BLOCK
                narrow(early.at[way, pl.ds(i * BLOCK, BLOCK)], first + i, left if way == 0 else right)

    @pl.when(y == 0)
    def _():
        pl.semaphore_wait(barrier, len(others))
        for k in range(1, zero):
            signal(opened, {"zero": k})

    @pl.when(y != 0)
    def _():
        pl.semaphore_wait(opened, 1)

    own_part.wait()
    arrived(column.at[pl.ds(0, zero - 1)], part_recv)
    own_row = pltpu.make_async_copy(column, table.at[bank], local_sem)
    own_row.start()
    own_row.wait()
    stages = [
        (bank, 1, [at_core(1)]),
        (bank - core, CORES, [at_x(k) for k in range(1, X)]),
        (chip_z * X * CORES, X * CORES, [at_z(k) for k in range(1, depth)]),
    ]

    def table_stage(s):
        if s:
            _, count, peers = stages[s - 1]
            arrived(table.at[pl.ds(0, count * len(peers))], table_recv.at[s - 1])
        if s < len(stages):
            first, count, peers = stages[s]
            at = table.at[pl.ds(first, count)]
            for peer in peers:
                remote(at, at, table_send, table_recv.at[s], {"bank": peer}).start()
        else:
            width = part.shape[1]
            for j in range(zero):
                router[:, j * width : (j + 1) * width] = table[:, j, 0, :].astype(jnp.bfloat16)

    for hop in (1, 2, 3, 4):
        for place in range(CHUNKS if hop < 4 else half):
            for way in (0, 1):
                ring(way, hop - 1, place).wait_recv()
                if hop < 3 or (hop == 3 and place < half):
                    ring(way, hop, place).start()
            if hop == 1:
                table_stage(place)

    for way in (0, 1):
        arrived(final.at[pl.ds(0, rows - EARLY * BLOCK), pl.ds(0, cols)], own_send.at[way])
        arrived(final.at[pl.ds(0, rows // 2), pl.ds(0, 5 * cols)], relay_send.at[way])
        if EARLY:
            send_early(way).wait_send()
    arrived(sums.at[pl.ds(0, zero - 1)], sum_send)
    arrived(column.at[pl.ds(0, zero - 1)], part_send)
    arrived(table.at[pl.ds(0, table.shape[0] - 1)], table_send)


def write(final, scale, router, final_out, scale_out, router_out, sem):
    copies = [
        pltpu.make_async_copy(final, final_out, sem.at[0]),
        pltpu.make_async_copy(router, router_out, sem.at[1]),
        pltpu.make_async_copy(scale, scale_out, sem.at[2]),
    ]
    for copy in copies:
        copy.start()
    for copy in copies:
        copy.wait()


def body(master_down, second_down, router_weight, router_gain):
    _, rows, cols = master_down.shape
    width = router_weight.shape[0]
    zero, banks = lax.axis_size("zero"), lax.axis_size("bank")
    f32, vmem, dma = jnp.float32, pltpu.VMEM, pltpu.SemaphoreType.DMA
    args = (
        master_down.reshape(rows, cols),
        second_down.reshape(rows, cols),
        router_weight.reshape(1, width),
        router_gain.reshape(1, width),
    )
    results = pl.pallas_call(
        kernel,
        out_shape=(
            jax.ShapeDtypeStruct((rows, zero * cols), jnp.bfloat16),
            jax.ShapeDtypeStruct((1, rows), f32),
            jax.ShapeDtypeStruct((banks, zero * width), jnp.bfloat16),
        ),
        in_specs=[pl.BlockSpec(memory_space=pltpu.HBM)] * 4,
        out_specs=[pl.BlockSpec(memory_space=vmem)] * 3,
        scratch_shapes=[
            vmem((rows, cols), f32),
            vmem((rows, cols), jnp.bfloat16),
            vmem((1, rows), f32),
            vmem((zero, 1, rows), f32),
            vmem((1, width), f32),
            vmem((1, width), f32),
            vmem((1, width), f32),
            vmem((zero, 1, width), f32),
            vmem((banks, zero, 1, width), f32),
            vmem((2, max(EARLY, 1) * BLOCK, cols), f32),
            pltpu.SemaphoreType.REGULAR,
            pltpu.SemaphoreType.REGULAR,
            dma((2,)),
            dma((2,)),
            dma(()),
            dma(()),
            dma(()),
            dma(()),
            dma(()),
            dma(()),
            dma((3,)),
            dma((2,)),
            dma((2,)),
            dma((2,)),
            dma((2,)),
            dma((2, 7 * CHUNKS // 2)),
        ],
        compiler_params=pltpu.CompilerParams(
            collective_id=0, has_side_effects=True, vmem_limit_bytes=40 * 2**20
        ),
        name="gather",
    )(*map(in_hbm, args))
    final, scale, router = pl.pallas_call(
        write,
        out_shape=tuple(jax.ShapeDtypeStruct(x.shape, x.dtype) for x in results),
        in_specs=[pl.BlockSpec(memory_space=pl.ANY)] * 3,
        out_specs=[pl.BlockSpec(memory_space=pl.ANY)] * 3,
        scratch_shapes=[dma((3,))],
        compiler_params=pltpu.CompilerParams(vmem_limit_bytes=2**20),
        name="write",
    )(*(pltpu.with_memory_space_constraint(x, vmem) for x in results))
    return final.reshape(1, rows, zero * cols), scale, router.T


def in_hbm(value):
    return pltpu.with_memory_space_constraint(value, pltpu.HBM)


def solution(mesh):
    return jax.shard_map(
        body,
        mesh=mesh,
        in_specs=(P("bank", None, "zero"), P("bank", None, "zero"), P("zero", "bank"), P("zero")),
        out_specs=(P("bank", None, None), P("bank", None), P()),
        check_vma=False,
    )
```

time: 115 us -> 70 us (0.61)
  Pallas kernels: 0 us -> 69.2 us
  waiting for transfers between devices: 43 us -> 0 us
  blocking collectives: 28.9 us -> 0 us
  starting transfers between devices: 14 us -> 0 us
  between operations: 14.1 us -> 0.64 us
  local copies, waits for them, and re-layouts: 9.55 us -> 0 us
  other arithmetic: 5.32 us -> 0 us
    pallas_call x0 -> x2, Pallas kernels: none -> 69.2 us  [the longest x1 66.6 us: body(): pl.pallas_call(kernel, out_shape=(jax.ShapeDtypeStruct((rows, zero * cols...]
    all_gather x1 -> x0, waiting for transfers between devices: 31.6 us -> none  [body(): final_down = lax.all_gather(narrow_down, 'zero', axis=2, tiled=True)]
    all_to_all x1 -> x0, blocking collectives: 15.1 us -> none  [from_everyone(): lax.all_to_all(jnp.broadcast_to(value[None], (size, *value.shape)), axis,...]
    all_to_all x1 -> x0, starting transfers between devices: 14 us -> none  [from_everyone(): lax.all_to_all(jnp.broadcast_to(value[None], (size, *value.shape)), axis,...]
    all_gather x1 -> x0, blocking collectives: 13.9 us -> none  [body(): row_router = lax.all_gather(part_router, 'zero', axis=0, tiled=True)]
    all_to_all x1 -> x0, waiting for transfers between devices: 11.3 us -> none  [from_everyone(): lax.all_to_all(jnp.broadcast_to(value[None], (size, *value.shape)), axis,...]
    unnamed x13 -> x0, local copies, waits for them, and re-layouts: 8.07 us -> none
    unnamed x1 -> x0, other arithmetic: 2.15 us -> none
  transfers between devices with their start and end apart: 2 -> 0, of which waited for: 2 -> 0; matrix products, arithmetic and copies ran while one was open for 5% -> 0% of each run, Pallas kernels for 0% -> 0%
where the time goes in v3:
time: 70 us; the launch traced here: 69.9 us
  Pallas kernels  69.2 us (99%)
    pallas_call x1, Pallas kernels, body(): pl.pallas_call(kernel, out_shape=(jax.ShapeDtypeStruct((rows, zero * cols...  66.6 us
    pallas_call x1, Pallas kernels, body(): pl.pallas_call(write, out_shape=tuple((jax.ShapeDtypeStruct(x.shape, x.dt...  2.63 us

profile of v3, /device:TPU:6, one launch (start us, length us, event | category | flops | bytes accessed | tf_op | source)
XLA Modules:
  0.0 69.9 jit_solution(1249280217272548400)
XLA Ops:
  0.6 66.6 %gather.1 = (bf16[1408,2048]{1,0:T(8,128)(2,1)S(1)}, f32[1,1408]{1,0:T(1,128)S(1)}, bf16[64,2048]{1,0:T(8,128)(2,1)S(1)}) custom-call(f32[1408,256]{1,0:T(8,128)} %bitcast.6, bf16[1408,256]{1,0:T(8,128)(2,1)} %bitcast.7, f32[1,256]{1,0:T(1,128)} %bitcast.8, f32[1,256]{1,0:T(1,128)} %bitcast.9), custom_call_target="tpu_custom_call" | custom-call | tf_op jit(solution)/shard_map/gather/pallas_call | solution.py:264
  67.2 2.6 %write.1 = (bf16[1408,2048]{1,0:T(8,128)(2,1)}, f32[1,1408]{1,0:T(1,128)}, bf16[64,2048]{1,0:T(8,128)(2,1)}) custom-call(bf16[1408,2048]{1,0:T(8,128)(2,1)S(1)} %get-tuple-element.9.final, f32[1,1408]{1,0:T(1,128)S(1)} %get-tuple-element.10.scale, bf16[64,2048]{1,0:T(8,128)(2,1)S(1)} %get-tuple-element.11.router), custom_call_target="tpu_custom_call" | custom-call | tf_op jit(solution)/shard_map/write/pallas_call | solution.py:306

commit v4 on v3

--- a/solution.py
+++ b/solution.py
@@ -7,9 +7,10 @@
 
 MESH = pl.DeviceIdType.MESH
 BLOCK = 128
-CHUNKS = 4
+HALVES = 2
+FIRST = 352
 LOADS = 4
-EARLY = 0
+EARLY = 128
 X, CORES = 4, 2
 
 
@@ -23,7 +24,7 @@
 ):
     rows, cols = merged.shape
     zero = lax.axis_size("zero")
-    blocks, chunk, half = rows // BLOCK, rows // CHUNKS, CHUNKS // 2
+    blocks, half = rows // BLOCK, rows // HALVES
     y, bank = lax.axis_index("zero"), lax.axis_index("bank")
     chip_z, chip_x = bank // (X * CORES), lax.rem(bank // CORES, X)
     depth = lax.axis_size("bank") // (X * CORES)
@@ -90,7 +91,7 @@
     def _():
         pl.semaphore_wait(barrier, zero - 1)
 
-    @pl.when(y == 1)
+    @pl.when(y == zero - 1)
     def _():
         signal(ready, {"zero": 0})
 
@@ -101,7 +102,7 @@
     left, right = lax.rem(y + zero - 1, zero), lax.rem(y + 1, zero)
 
     def early_rows(way):
-        return pl.ds(0 if way == 0 else rows - EARLY * BLOCK, EARLY * BLOCK)
+        return pl.ds(0 if way == 0 else rows - EARLY, EARLY)
 
     def send_early(way):
         return remote(
@@ -136,69 +137,50 @@
     def columns(owner):
         return pl.ds(pl.multiple_of(owner * cols, cols), cols)
 
-    def narrow(source, block, owner):
-        at = slice(block * BLOCK, (block + 1) * BLOCK)
-        tall = jnp.broadcast_to(inverse[:, at], (BLOCK, BLOCK)).T
-        wide = jnp.concatenate([tall] * (cols // 128), axis=1)
-        final[at, columns(owner)] = (source[...] * wide).astype(jnp.bfloat16)
-
-    def ring(way, hop, place):
-        c = place if way == 0 else CHUNKS - 1 - place
-        start, count = c * chunk, chunk
-        if hop == 0 and place == 0:
-            start, count = start + (EARLY * BLOCK if way == 0 else 0), count - EARLY * BLOCK
+    def narrow(source, start, count, owner):
+        block = start // BLOCK * BLOCK
+        tall = jnp.broadcast_to(inverse[:, block : block + BLOCK], (BLOCK, BLOCK)).T
+        wide = jnp.concatenate([tall[start - block : start - block + count]] * (cols // 128), axis=1)
+        final[start : start + count, columns(owner)] = (source[...] * wide).astype(jnp.bfloat16)
+
+    def ring(way, hop, place, first=0, last=half):
+        if way == 0:
+            start = place * half + first
+        else:
+            start = rows - place * half - last
         owner = lax.rem(y + (zero - hop if way == 0 else hop), zero)
-        at = final.at[pl.ds(start, count), columns(owner)]
+        at = final.at[pl.ds(start, last - first), columns(owner)]
         sem = own_send if hop == 0 else relay_send
         return remote(
-            at, at, sem.at[way], ring_recv.at[way, hop * CHUNKS + place],
+            at, at, sem.at[way], ring_recv.at[way, hop * HALVES + place],
             {"zero": right if way == 0 else left},
         )
 
-    mine = list(range(EARLY, blocks - EARLY))
-    order = []
-    for place in range(CHUNKS):
+    done, waiting = set(), None
+
+    def own(start, stop):
+        for i in range(start // BLOCK, -(-stop // BLOCK)):
+            if i not in done:
+                done.add(i)
+                narrow(merged.at[pl.ds(i * BLOCK, BLOCK)], i * BLOCK, BLOCK, y)
+
+    for place, first, last in ((0, EARLY, FIRST), (0, FIRST, half), (1, 0, FIRST), (1, FIRST, half)):
         for way in (0, 1):
-            c = place if way == 0 else CHUNKS - 1 - place
-            need = [i for i in mine if i * BLOCK < (c + 1) * chunk and (i + 1) * BLOCK > c * chunk]
-            order.append(([i for i in need if all(i not in o[0] for o in order)], way, place))
-    waiting = None
-    for need, way, place in order:
-        for i in need:
-            narrow(merged.at[pl.ds(i * BLOCK, BLOCK)], i, y)
-        if waiting and need:
-            ring(*waiting).start()
-            waiting = None
-        elif waiting:
-            ring(*waiting).start()
-        waiting = (way, 0, place)
-    for i in range(blocks):
-        if i not in mine:
-            narrow(merged.at[pl.ds(i * BLOCK, BLOCK)], i, y)
-    ring(*waiting).start()
+            start, stop = place * half + first, place * half + last
+            own(*((start, stop) if way == 0 else (rows - stop, rows - start)))
+            if waiting:
+                ring(*waiting).start()
+            waiting = (way, 0, place, first, last)
+    own(0, rows)
 
     if EARLY:
         for way in (0, 1):
             send_early(way).wait_recv()
-            for i in range(EARLY):
-                first = early_rows(way).start // BLOCK
-                narrow(early.at[way, pl.ds(i * BLOCK, BLOCK)], first + i, left if way == 0 else right)
-
-    @pl.when(y == 0)
-    def _():
-        pl.semaphore_wait(barrier, len(others))
-        for k in range(1, zero):
-            signal(opened, {"zero": k})
-
-    @pl.when(y != 0)
-    def _():
-        pl.semaphore_wait(opened, 1)
-
-    own_part.wait()
-    arrived(column.at[pl.ds(0, zero - 1)], part_recv)
-    own_row = pltpu.make_async_copy(column, table.at[bank], local_sem)
-    own_row.start()
-    own_row.wait()
+            first = early_rows(way).start
+            for start in range(first, first + EARLY, 64):
+                narrow(early.at[way, pl.ds(start - first, 64)], start, 64, left if way == 0 else right)
+    ring(*waiting).start()
+
     stages = [
         (bank, 1, [at_core(1)]),
         (bank - core, CORES, [at_x(k) for k in range(1, X)]),
@@ -209,6 +191,12 @@
         if s:
             _, count, peers = stages[s - 1]
             arrived(table.at[pl.ds(0, count * len(peers))], table_recv.at[s - 1])
+        else:
+            own_part.wait()
+            arrived(column.at[pl.ds(0, zero - 1)], part_recv)
+            own_row = pltpu.make_async_copy(column, table.at[bank], local_sem)
+            own_row.start()
+            own_row.wait()
         if s < len(stages):
             first, count, peers = stages[s]
             at = table.at[pl.ds(first, count)]
@@ -219,17 +207,39 @@
             for j in range(zero):
                 router[:, j * width : (j + 1) * width] = table[:, j, 0, :].astype(jnp.bfloat16)
 
+    def open_gate():
+        @pl.when(y == 0)
+        def _():
+            pl.semaphore_wait(barrier, len(others))
+            for k in range(1, zero):
+                signal(opened, {"zero": k})
+
+    def pass_gate():
+        @pl.when(y != 0)
+        def _():
+            pl.semaphore_wait(opened, 1)
+
+        table_stage(0)
+
+    between = {
+        (1, 0): open_gate,
+        (1, 1): pass_gate,
+        (2, 0): lambda: table_stage(1),
+        (2, 1): lambda: table_stage(2),
+        (3, 0): lambda: table_stage(3),
+    }
     for hop in (1, 2, 3, 4):
-        for place in range(CHUNKS if hop < 4 else half):
+        for place in range(HALVES if hop < 4 else 1):
             for way in (0, 1):
-                ring(way, hop - 1, place).wait_recv()
-                if hop < 3 or (hop == 3 and place < half):
+                arrival = ring(way, hop - 1, place, EARLY if (hop, place) == (1, 0) else 0)
+                arrival.wait_recv()
+                if hop < 3 or (hop == 3 and place == 0):
                     ring(way, hop, place).start()
-            if hop == 1:
-                table_stage(place)
+            if (hop, place) in between:
+                between[hop, place]()
 
     for way in (0, 1):
-        arrived(final.at[pl.ds(0, rows - EARLY * BLOCK), pl.ds(0, cols)], own_send.at[way])
+        arrived(final.at[pl.ds(0, rows - EARLY), pl.ds(0, cols)], own_send.at[way])
         arrived(final.at[pl.ds(0, rows // 2), pl.ds(0, 5 * cols)], relay_send.at[way])
         if EARLY:
             send_early(way).wait_send()
@@ -280,7 +290,7 @@
             vmem((1, width), f32),
             vmem((zero, 1, width), f32),
             vmem((banks, zero, 1, width), f32),
-            vmem((2, max(EARLY, 1) * BLOCK, cols), f32),
+            vmem((2, max(EARLY, 8), cols), f32),
             pltpu.SemaphoreType.REGULAR,
             pltpu.SemaphoreType.REGULAR,
             dma((2,)),
@@ -296,7 +306,7 @@
             dma((2,)),
             dma((2,)),
             dma((2,)),
-            dma((2, 7 * CHUNKS // 2)),
+            dma((2, 3 * HALVES + 1)),
         ],
         compiler_params=pltpu.CompilerParams(
             collective_id=0, has_side_effects=True, vmem_limit_bytes=40 * 2**20

time: 70 us -> 69 us (0.986)
  Pallas kernels: 69.2 us -> 67.6 us
    pallas_call x1, Pallas kernels: 66.6 us -> 65 us  [body(): pl.pallas_call(kernel, out_shape=(jax.ShapeDtypeStruct((rows, zero * cols...]
where the time goes in v4:
time: 69 us; the launch traced here: 68.2 us
  Pallas kernels  67.6 us (98%)
    pallas_call x1, Pallas kernels, body(): pl.pallas_call(kernel, out_shape=(jax.ShapeDtypeStruct((rows, zero * cols...  65 us
    pallas_call x1, Pallas kernels, body(): pl.pallas_call(write, out_shape=tuple((jax.ShapeDtypeStruct(x.shape, x.dt...  2.63 us

profile of v4, /device:TPU:6, one launch (start us, length us, event | category | flops | bytes accessed | tf_op | source)
XLA Modules:
  0.0 68.2 jit_solution(4806085958569050566)
XLA Ops:
  0.6 65.0 %gather.1 = (bf16[1408,2048]{1,0:T(8,128)(2,1)S(1)}, f32[1,1408]{1,0:T(1,128)S(1)}, bf16[64,2048]{1,0:T(8,128)(2,1)S(1)}) custom-call(f32[1408,256]{1,0:T(8,128)} %bitcast.6, bf16[1408,256]{1,0:T(8,128)(2,1)} %bitcast.7, f32[1,256]{1,0:T(1,128)} %bitcast.8, f32[1,256]{1,0:T(1,128)} %bitcast.9), custom_call_target="tpu_custom_call" | custom-call | tf_op jit(solution)/shard_map/gather/pallas_call | solution.py:274
  65.6 2.6 %write.1 = (bf16[1408,2048]{1,0:T(8,128)(2,1)}, f32[1,1408]{1,0:T(1,128)}, bf16[64,2048]{1,0:T(8,128)(2,1)}) custom-call(bf16[1408,2048]{1,0:T(8,128)(2,1)S(1)} %get-tuple-element.9.final, f32[1,1408]{1,0:T(1,128)S(1)} %get-tuple-element.10.scale, bf16[64,2048]{1,0:T(8,128)(2,1)S(1)} %get-tuple-element.11.router), custom_call_target="tpu_custom_call" | custom-call | tf_op jit(solution)/shard_map/write/pallas_call | solution.py:316

commit v5 on v4

--- a/solution.py
+++ b/solution.py
@@ -11,6 +11,8 @@
 FIRST = 352
 LOADS = 4
 EARLY = 128
+LEAST = 0
+GATE, HERALD = 7, 6
 X, CORES = 4, 2
 
 
@@ -20,7 +22,7 @@
     merged, added, own_sum, sums, w_v, g_v, part, column, table, early,
     ready, opened, load_sem, small_sem, local_sem,
     sum_send, sum_recv, part_send, part_recv, table_send, table_recv,
-    early_send, early_recv, own_send, relay_send, ring_recv,
+    early_send, early_recv, ring_send, ring_recv,
 ):
     rows, cols = merged.shape
     zero = lax.axis_size("zero")
@@ -54,7 +56,7 @@
     for k in range(1, zero):
         peer = lax.rem(y + k, zero)
 
-        @pl.when(peer != 0)
+        @pl.when(peer != GATE)
         def _(peer=peer):
             signal(barrier, {"zero": peer})
 
@@ -87,34 +89,41 @@
         copy.wait()
     part[...] = (w_v[...] * g_v[...]).astype(jnp.bfloat16).astype(jnp.float32)
 
-    @pl.when(y != 0)
+    @pl.when(y != GATE)
     def _():
         pl.semaphore_wait(barrier, zero - 1)
 
-    @pl.when(y == zero - 1)
+    @pl.when(y == HERALD)
     def _():
-        signal(ready, {"zero": 0})
-
-    @pl.when(y == 0)
+        signal(ready, {"zero": GATE})
+
+    @pl.when(y == GATE)
     def _():
         pl.semaphore_wait(ready, 1)
 
     left, right = lax.rem(y + zero - 1, zero), lax.rem(y + 1, zero)
 
-    def early_rows(way):
-        return pl.ds(0 if way == 0 else rows - EARLY, EARLY)
-
-    def send_early(way):
+    def by_ring(act):
+        for late, count in ((True, LEAST), (False, EARLY)):
+
+            @pl.when((bank == 0) == late)
+            def _(count=count):
+                act(count)
+
+    def send_early(way, count):
+        first = 0 if way == 0 else rows - count
         return remote(
-            merged.at[early_rows(way)], early.at[way], early_send.at[way], early_recv.at[way],
+            merged.at[pl.ds(first, count)], early.at[way, pl.ds(0, count)], early_send, early_recv.at[way],
             {"zero": right if way == 0 else left},
         )
 
+    def start_early(count):
+        for way in (0, 1) if count else ():
+            send_early(way, count).start()
+
     for k in (4, 3, 5, 2, 6, 1, 7):
         remote(own_sum, sums.at[y], sum_send, sum_recv, {"zero": lax.rem(y + k, zero)}).start()
-    if EARLY:
-        for way in (0, 1):
-            send_early(way).start()
+    by_ring(start_early)
     for k in range(1, zero):
         remote(part, column.at[y], part_send, part_recv, {"zero": lax.rem(y + k, zero)}).start()
     own_part = pltpu.make_async_copy(part, column.at[y], local_sem)
@@ -124,7 +133,7 @@
     others += [at_x(k) for k in range(1, X)]
     others += [at_z(k) for k in range(1, depth)]
 
-    @pl.when(y == 0)
+    @pl.when(y == GATE)
     def _():
         for peer in others:
             signal(barrier, {"bank": peer})
@@ -150,9 +159,8 @@
             start = rows - place * half - last
         owner = lax.rem(y + (zero - hop if way == 0 else hop), zero)
         at = final.at[pl.ds(start, last - first), columns(owner)]
-        sem = own_send if hop == 0 else relay_send
         return remote(
-            at, at, sem.at[way], ring_recv.at[way, hop * HALVES + place],
+            at, at, ring_send.at[way], ring_recv.at[way, hop * HALVES + place],
             {"zero": right if way == 0 else left},
         )
 
@@ -164,22 +172,30 @@
                 done.add(i)
                 narrow(merged.at[pl.ds(i * BLOCK, BLOCK)], i * BLOCK, BLOCK, y)
 
-    for place, first, last in ((0, EARLY, FIRST), (0, FIRST, half), (1, 0, FIRST), (1, FIRST, half)):
+    def send_own(way, place, first, last):
+        if (place, first) == (0, LEAST):
+            by_ring(lambda count: ring(way, 0, place, count, last).start())
+        else:
+            ring(way, 0, place, first, last).start()
+
+    for place, first, last in ((0, LEAST, FIRST), (0, FIRST, half), (1, 0, FIRST), (1, FIRST, half)):
         for way in (0, 1):
             start, stop = place * half + first, place * half + last
             own(*((start, stop) if way == 0 else (rows - stop, rows - start)))
             if waiting:
-                ring(*waiting).start()
-            waiting = (way, 0, place, first, last)
+                send_own(*waiting)
+            waiting = (way, place, first, last)
     own(0, rows)
 
-    if EARLY:
-        for way in (0, 1):
-            send_early(way).wait_recv()
-            first = early_rows(way).start
-            for start in range(first, first + EARLY, 64):
-                narrow(early.at[way, pl.ds(start - first, 64)], start, 64, left if way == 0 else right)
-    ring(*waiting).start()
+    def take_early(count):
+        for way in (0, 1) if count else ():
+            send_early(way, count).wait_recv()
+            first = 0 if way == 0 else rows - count
+            for i in range(0, count, 64):
+                narrow(early.at[way, pl.ds(i, 64)], first + i, 64, left if way == 0 else right)
+
+    by_ring(take_early)
+    send_own(*waiting)
 
     stages = [
         (bank, 1, [at_core(1)]),
@@ -208,14 +224,14 @@
                 router[:, j * width : (j + 1) * width] = table[:, j, 0, :].astype(jnp.bfloat16)
 
     def open_gate():
-        @pl.when(y == 0)
+        @pl.when(y == GATE)
         def _():
             pl.semaphore_wait(barrier, len(others))
             for k in range(1, zero):
-                signal(opened, {"zero": k})
+                signal(opened, {"zero": (GATE + k) % zero})
 
     def pass_gate():
-        @pl.when(y != 0)
+        @pl.when(y != GATE)
         def _():
             pl.semaphore_wait(opened, 1)
 
@@ -231,18 +247,22 @@
     for hop in (1, 2, 3, 4):
         for place in range(HALVES if hop < 4 else 1):
             for way in (0, 1):
-                arrival = ring(way, hop - 1, place, EARLY if (hop, place) == (1, 0) else 0)
-                arrival.wait_recv()
+                if (hop, place) == (1, 0):
+                    by_ring(lambda count: ring(way, 0, 0, count).wait_recv())
+                else:
+                    ring(way, hop - 1, place).wait_recv()
                 if hop < 3 or (hop == 3 and place == 0):
                     ring(way, hop, place).start()
             if (hop, place) in between:
                 between[hop, place]()
 
-    for way in (0, 1):
-        arrived(final.at[pl.ds(0, rows - EARLY), pl.ds(0, cols)], own_send.at[way])
-        arrived(final.at[pl.ds(0, rows // 2), pl.ds(0, 5 * cols)], relay_send.at[way])
-        if EARLY:
-            send_early(way).wait_send()
+    def ring_left(count):
+        for way in (0, 1):
+            arrived(final.at[pl.ds(0, (rows * 7 // 2 - count) // 4), pl.ds(0, 4 * cols)], ring_send.at[way])
+        if count:
+            arrived(early.at[pl.ds(0, 2 * count // EARLY)], early_send)
+
+    by_ring(ring_left)
     arrived(sums.at[pl.ds(0, zero - 1)], sum_send)
     arrived(column.at[pl.ds(0, zero - 1)], part_send)
     arrived(table.at[pl.ds(0, table.shape[0] - 1)], table_send)
@@ -290,7 +310,7 @@
             vmem((1, width), f32),
             vmem((zero, 1, width), f32),
             vmem((banks, zero, 1, width), f32),
-            vmem((2, max(EARLY, 8), cols), f32),
+            vmem((2, EARLY, cols), f32),
             pltpu.SemaphoreType.REGULAR,
             pltpu.SemaphoreType.REGULAR,
             dma((2,)),
@@ -302,8 +322,7 @@
             dma(()),
             dma(()),
             dma((3,)),
-            dma((2,)),
-            dma((2,)),
+            dma(()),
             dma((2,)),
             dma((2,)),
             dma((2, 3 * HALVES + 1)),

time: 69 us -> 68.2 us (0.988)
  no operation moved by 1% of the time
where the time goes in v5:
time: 68.2 us; the launch traced here: 67.9 us
  Pallas kernels  67.3 us (99%)
    pallas_call x1, Pallas kernels, body(): pl.pallas_call(kernel, out_shape=(jax.ShapeDtypeStruct((rows, zero * cols...  64.6 us
    pallas_call x1, Pallas kernels, body(): pl.pallas_call(write, out_shape=tuple((jax.ShapeDtypeStruct(x.shape, x.dt...  2.63 us

profile of v5, /device:TPU:6, one launch (start us, length us, event | category | flops | bytes accessed | tf_op | source)
XLA Modules:
  0.0 67.9 jit_solution(14253216277833797837)
XLA Ops:
  0.6 64.6 %gather.1 = (bf16[1408,2048]{1,0:T(8,128)(2,1)S(1)}, f32[1,1408]{1,0:T(1,128)S(1)}, bf16[64,2048]{1,0:T(8,128)(2,1)S(1)}) custom-call(f32[1408,256]{1,0:T(8,128)} %bitcast.6, bf16[1408,256]{1,0:T(8,128)(2,1)} %bitcast.7, f32[1,256]{1,0:T(1,128)} %bitcast.8, f32[1,256]{1,0:T(1,128)} %bitcast.9), custom_call_target="tpu_custom_call" | custom-call | tf_op jit(solution)/shard_map/gather/pallas_call | solution.py:294
  65.3 2.6 %write.1 = (bf16[1408,2048]{1,0:T(8,128)(2,1)}, f32[1,1408]{1,0:T(1,128)}, bf16[64,2048]{1,0:T(8,128)(2,1)}) custom-call(bf16[1408,2048]{1,0:T(8,128)(2,1)S(1)} %get-tuple-element.9.final, f32[1,1408]{1,0:T(1,128)S(1)} %get-tuple-element.10.scale, bf16[64,2048]{1,0:T(8,128)(2,1)S(1)} %get-tuple-element.11.router), custom_call_target="tpu_custom_call" | custom-call | tf_op jit(solution)/shard_map/write/pallas_call | solution.py:335

commit v6 on v5

--- a/solution.py
+++ b/solution.py
@@ -53,7 +53,7 @@
         )
 
     barrier = pltpu.get_barrier_semaphore()
-    for k in range(1, zero):
+    for k in (4, 3, 5, 2, 6, 1, 7):
         peer = lax.rem(y + k, zero)
 
         @pl.when(peer != GATE)
@@ -164,27 +164,30 @@
             {"zero": right if way == 0 else left},
         )
 
-    done, waiting = set(), None
+    def send_own(way, place, first, last):
+        if (place, first) == (0, LEAST):
+            by_ring(lambda count: ring(way, 0, place, count, last).start())
+        else:
+            ring(way, 0, place, first, last).start()
+
+    done, queue = set(), []
+
+    def follow():
+        while queue:
+            send_own(*queue.pop(0))
 
     def own(start, stop):
         for i in range(start // BLOCK, -(-stop // BLOCK)):
             if i not in done:
                 done.add(i)
                 narrow(merged.at[pl.ds(i * BLOCK, BLOCK)], i * BLOCK, BLOCK, y)
-
-    def send_own(way, place, first, last):
-        if (place, first) == (0, LEAST):
-            by_ring(lambda count: ring(way, 0, place, count, last).start())
-        else:
-            ring(way, 0, place, first, last).start()
+                follow()
 
     for place, first, last in ((0, LEAST, FIRST), (0, FIRST, half), (1, 0, FIRST), (1, FIRST, half)):
         for way in (0, 1):
             start, stop = place * half + first, place * half + last
             own(*((start, stop) if way == 0 else (rows - stop, rows - start)))
-            if waiting:
-                send_own(*waiting)
-            waiting = (way, place, first, last)
+            queue.append((way, place, first, last))
     own(0, rows)
 
     def take_early(count):
@@ -195,7 +198,7 @@
                 narrow(early.at[way, pl.ds(i, 64)], first + i, 64, left if way == 0 else right)
 
     by_ring(take_early)
-    send_own(*waiting)
+    follow()
 
     stages = [
         (bank, 1, [at_core(1)]),

time: 68.2 us -> 68.2 us (level)
  no operation moved by 1% of the time
where the time goes in v6:
time: 68.2 us; the launch traced here: 67.9 us
  Pallas kernels  67.2 us (99%)
    pallas_call x1, Pallas kernels, body(): pl.pallas_call(kernel, out_shape=(jax.ShapeDtypeStruct((rows, zero * cols...  64.6 us
    pallas_call x1, Pallas kernels, body(): pl.pallas_call(write, out_shape=tuple((jax.ShapeDtypeStruct(x.shape, x.dt...  2.63 us

profile of v6, /device:TPU:6, one launch (start us, length us, event | category | flops | bytes accessed | tf_op | source)
XLA Modules:
  0.0 67.9 jit_solution(4442066012366303801)
XLA Ops:
  0.6 64.6 %gather.1 = (bf16[1408,2048]{1,0:T(8,128)(2,1)S(1)}, f32[1,1408]{1,0:T(1,128)S(1)}, bf16[64,2048]{1,0:T(8,128)(2,1)S(1)}) custom-call(f32[1408,256]{1,0:T(8,128)} %bitcast.6, bf16[1408,256]{1,0:T(8,128)(2,1)} %bitcast.7, f32[1,256]{1,0:T(1,128)} %bitcast.8, f32[1,256]{1,0:T(1,128)} %bitcast.9), custom_call_target="tpu_custom_call" | custom-call | tf_op jit(solution)/shard_map/gather/pallas_call | solution.py:297
  65.3 2.6 %write.1 = (bf16[1408,2048]{1,0:T(8,128)(2,1)}, f32[1,1408]{1,0:T(1,128)}, bf16[64,2048]{1,0:T(8,128)(2,1)}) custom-call(bf16[1408,2048]{1,0:T(8,128)(2,1)S(1)} %get-tuple-element.9.final, f32[1,1408]{1,0:T(1,128)S(1)} %get-tuple-element.10.scale, bf16[64,2048]{1,0:T(8,128)(2,1)S(1)} %get-tuple-element.11.router), custom_call_target="tpu_custom_call" | custom-call | tf_op jit(solution)/shard_map/write/pallas_call | solution.py:338
